TPU v7x, 32 devices: a whole 2x2x4 slice. The times are simulated.
32 devices in a mesh: prow: 4 (over z), pcol: 8 (over y, x, core).
Axes of the slice: x: 2, y: 2, z: 4, core: 2. Of those that a mesh axis runs over, the one named last changes fastest.
Arguments:
- tiles: bfloat16 [4, 8, 32, 256, 256], P('prow', 'pcol')
- tile_brow: int32 [4, 8, 32], P('prow', 'pcol'), may hold values from 0 to 31, as said below
- tile_bcol: int32 [4, 8, 32], P('prow', 'pcol'), may hold values from 0 to 15, as said below
- tile_count: int32 [4, 8], P('prow', 'pcol'), may hold values from 8 to 32, as said below
Outputs:
- row_scale: float32 [32, 4, 256], P(None, 'prow')
- col_scale: float32 [16, 8, 256], P(None, 'pcol')
Inputs may be any that keep to these rules, and one draw needn't show every extreme that they name: `tile_brow`: on one device, no two slots name the same pair of local block row and column; the diagonal tile of every block row is present and live, in the first slots of the device that holds it. `tile_bcol`: see tile_brow. `tile_count`: a device that holds diagonal tiles has all 32 slots live, every other device at most 16.
All inputs are finite; a program needn't handle non-finite values.
Results may differ from a plain program's by a relative error of at most 0.0003.
Values sent between devices are 32-bit elements; how exact they have to be, the bound alone decides.
A program may use at most 64 MiB of HBM per device.

v0:
```python
import functools

import jax
import jax.numpy as jnp
from jax import lax
from jax.experimental import pallas as pl
from jax.experimental.pallas import tpu as pltpu
from jax.sharding import PartitionSpec as P

BR_DEV = 32
SWEEPS = 3
LANES = 128
STEP = 4
ROWS = 16


def rescale(scale, largest):
    return scale / jnp.sqrt(largest)


def kernel(
    n_prow, n_pcol, col_blocks, slots, width,
    brow_ref, bcol_ref, count_ref, tiles_ref,
    row_out, col_out,
    block, row_split, col_vec, spread_a, spread_b, peak_a, peak_b,
    row_send, part_recv, done_send, done_recv, col_send, col_recv,
    load_sem, part_send_sem, part_recv_sem,
    done_send_sem, done_recv_sem, col_send_sem, col_recv_sem,
):
    def load(t):
        at = pl.ds(t * STEP, STEP)
        return pltpu.make_async_copy(tiles_ref.at[at], block.at[at], load_sem.at[t])

    for t in range(slots // STEP):
        load(t).start()

    pr = lax.axis_index("prow")
    pc = lax.axis_index("pcol")
    barrier = pltpu.get_barrier_semaphore()
    for d in range(1, n_pcol):
        pl.semaphore_signal(barrier, inc=1, device_id={"pcol": lax.rem(pc + d, n_pcol)})
    for d in range(1, n_prow):
        pl.semaphore_signal(barrier, inc=1, device_id={"prow": lax.rem(pr + d, n_prow)})

    count = count_ref[0]
    row_ids = lax.broadcasted_iota(jnp.int32, (BR_DEV, width), 0)
    col_ids = lax.broadcasted_iota(jnp.int32, (col_blocks, width), 0)
    lane_ids = lax.broadcasted_iota(jnp.int32, (1, LANES), 1)
    ones = jnp.ones((LANES, LANES), jnp.bfloat16)
    lane_full = lax.broadcasted_iota(jnp.int32, (8, LANES), 1)
    lane_group = lane_full // 8
    own_lane = lane_full % 8 == lax.broadcasted_iota(jnp.int32, (8, LANES), 0)
    halves = width // LANES
    peak_b[...] = jnp.zeros_like(peak_b)

    def spread_rows(s, out, j):
        brow = brow_ref[jnp.minimum(s, slots - 1)]
        pick = jnp.where(
            (lane_ids % BR_DEV == brow) & (lane_ids < 3 * BR_DEV), 1.0, 0.0
        ).astype(jnp.bfloat16)
        out[j] = jnp.dot(row_split[...] * pick, ones, preferred_element_type=jnp.float32)

    def scale_tile(s, spread, peak, j, col_acc):
        bcol = bcol_ref[s]
        if spread is not None:
            cols = col_vec[pl.ds(bcol, 1), :]
        col_part = [None] * halves
        for g in range(width // ROWS):
            at = slice(g * ROWS, (g + 1) * ROWS)
            best = None
            for h in range(halves):
                lanes = slice(h * LANES, (h + 1) * LANES)
                x = jnp.abs(block[s, at, lanes]).astype(jnp.float32)
                if spread is not None:
                    x = (x * spread[j, at, :]) * cols[:, lanes]
                col_part[h] = x if g == 0 else jnp.maximum(col_part[h], x)
                best = x if h == 0 else jnp.maximum(best, x)
            peak[j, at, :] = best
        top = jnp.concatenate([jnp.max(c, axis=0, keepdims=True) for c in col_part], axis=1)
        col_at = jnp.where(s < count, bcol, -1)
        return jnp.maximum(col_acc, jnp.where(col_ids == col_at, top, 0.0))

    def reduce_rows(s, peak, j, row_acc):
        parts = []
        for h in range(halves):
            packed = None
            for g in range(LANES // 8):
                at = h * LANES + 8 * g
                best = jnp.max(peak[j, at:at + 8, :], axis=1, keepdims=True)
                best = jnp.broadcast_to(best, (8, LANES))
                packed = best if g == 0 else jnp.where(lane_group == g, best, packed)
            parts.append(jnp.max(jnp.where(own_lane, packed, 0.0), axis=0, keepdims=True))
        row_at = jnp.where((s >= 0) & (s < count), brow_ref[jnp.maximum(s, 0)], -1)
        return jnp.maximum(
            row_acc, jnp.where(row_ids == row_at, jnp.concatenate(parts, axis=1), 0.0)
        )

    def four_tiles(t, carry, first):
        row_acc, col_acc = carry
        base = t * STEP
        if first:
            load(t).wait()
        for part in range(2):
            here, peak = (spread_a, peak_a) if part == 0 else (spread_b, peak_b)
            there, last = (spread_b, peak_b) if part == 0 else (spread_a, peak_a)
            s = base + 2 * part
            if not first:
                for j in range(2):
                    spread_rows(s + 2 + j, there, j)
            for j in range(2):
                row_acc = reduce_rows(s - 2 + j, last, j, row_acc)
            for j in range(2):
                col_acc = scale_tile(s + j, None if first else here, peak, j, col_acc)
        return row_acc, col_acc

    row_vec = jnp.ones((BR_DEV, width), jnp.float32)
    col_now = jnp.ones((col_blocks, width), jnp.float32)
    share = BR_DEV // n_pcol
    for sweep in range(SWEEPS):
        if sweep > 0:
            for j in range(2):
                spread_rows(j, spread_a, j)
        row_max, col_max = lax.fori_loop(
            0, slots // STEP, functools.partial(four_tiles, first=sweep == 0),
            (jnp.zeros((BR_DEV, width), jnp.float32), jnp.zeros((col_blocks, width), jnp.float32)),
        )
        col_send[sweep] = col_max
        for j in range(2):
            row_max = reduce_rows(slots - 2 + j, peak_b, j, row_max)
        row_send[sweep] = row_max
        if sweep == 0:
            pl.semaphore_wait(barrier, n_pcol - 1 + n_prow - 1)
        part_copies = []
        for d in range(1, n_pcol):
            to = lax.rem(pc + d, n_pcol)
            part_copies.append(pltpu.make_async_remote_copy(
                src_ref=row_send.at[sweep], dst_ref=part_recv.at[sweep, d - 1],
                send_sem=part_send_sem.at[sweep, d - 1], recv_sem=part_recv_sem.at[sweep, d - 1],
                device_id={"pcol": to},
            ))
        for copy in part_copies:
            copy.start()
        col_copies = []
        for d in range(1, n_prow):
            col_copies.append(pltpu.make_async_remote_copy(
                src_ref=col_send.at[sweep], dst_ref=col_recv.at[sweep, d - 1],
                send_sem=col_send_sem.at[sweep, d - 1], recv_sem=col_recv_sem.at[sweep, d - 1],
                device_id={"prow": lax.rem(pr + d, n_prow)},
            ))
        for copy in col_copies:
            copy.start()
        for d, copy in enumerate(col_copies):
            copy.wait()
            col_max = jnp.maximum(col_max, col_recv[sweep, d])
        col_now = rescale(col_now, col_max)
        for d, copy in enumerate(part_copies):
            copy.wait()
            row_max = jnp.maximum(row_max, part_recv[sweep, d])
        row_vec = rescale(row_vec, row_max)
        if sweep + 1 < SWEEPS:
            col_vec[...] = col_now
            top = row_vec.astype(jnp.bfloat16).astype(jnp.float32)
            left = row_vec - top
            mid = left.astype(jnp.bfloat16).astype(jnp.float32)
            low = left - mid
            rest = jnp.zeros((LANES - 3 * BR_DEV, width), jnp.float32)
            stack = jnp.concatenate([top, mid, low, rest], axis=0)
            for h in range(halves):
                row_split[h * LANES:(h + 1) * LANES, :] = (
                    stack[:, h * LANES:(h + 1) * LANES].T.astype(jnp.bfloat16)
                )
    row_out[...] = row_vec
    col_out[...] = col_now


def spell(row_ref, col_ref, row_out, col_out):
    for ref, out in ((row_ref, row_out), (col_ref, col_out)):
        for i in range(ref.shape[0]):
            out[i] = ref[i:i + 1, :]


def solution(mesh):
    n_prow, n_pcol = mesh.shape["prow"], mesh.shape["pcol"]

    def on_device(tiles, tile_brow, tile_bcol, tile_count):
        slots, width = tiles.shape[2], tiles.shape[3]
        col_blocks = BR_DEV * n_prow // n_pcol
        share = BR_DEV // n_pcol
        smem = pl.BlockSpec(memory_space=pltpu.SMEM)
        vmem = pl.BlockSpec(memory_space=pltpu.VMEM)
        row_vec, col_vec = pl.pallas_call(
            functools.partial(kernel, n_prow, n_pcol, col_blocks, slots, width),
            out_shape=(
                jax.ShapeDtypeStruct((BR_DEV, width), jnp.float32),
                jax.ShapeDtypeStruct((col_blocks, width), jnp.float32),
            ),
            in_specs=[smem, smem, smem, pl.BlockSpec(memory_space=pl.ANY)],
            out_specs=(vmem, vmem),
            scratch_shapes=[
                pltpu.VMEM((slots, width, width), jnp.bfloat16),
                pltpu.VMEM((width, LANES), jnp.bfloat16),
                pltpu.VMEM((col_blocks, width), jnp.float32),
                pltpu.VMEM((2, width, LANES), jnp.float32),
                pltpu.VMEM((2, width, LANES), jnp.float32),
                pltpu.VMEM((2, width, LANES), jnp.float32),
                pltpu.VMEM((2, width, LANES), jnp.float32),
                pltpu.VMEM((SWEEPS, BR_DEV, width), jnp.float32),
                pltpu.VMEM((SWEEPS, n_pcol - 1, BR_DEV, width), jnp.float32),
                pltpu.VMEM((SWEEPS, share, width), jnp.float32),
                pltpu.VMEM((SWEEPS, n_pcol, share, width), jnp.float32),
                pltpu.VMEM((SWEEPS, col_blocks, width), jnp.float32),
                pltpu.VMEM((SWEEPS, n_prow - 1, col_blocks, width), jnp.float32),
                pltpu.SemaphoreType.DMA((slots // STEP,)),
                pltpu.SemaphoreType.DMA((SWEEPS, n_pcol - 1)),
                pltpu.SemaphoreType.DMA((SWEEPS, n_pcol - 1)),
                pltpu.SemaphoreType.DMA((SWEEPS, n_pcol - 1)),
                pltpu.SemaphoreType.DMA((SWEEPS, n_pcol - 1)),
                pltpu.SemaphoreType.DMA((SWEEPS, n_prow - 1)),
                pltpu.SemaphoreType.DMA((SWEEPS, n_prow - 1)),
            ],
            compiler_params=pltpu.CompilerParams(collective_id=0, has_side_effects=True),
        )(
            tile_brow.reshape(slots), tile_bcol.reshape(slots), tile_count.reshape(1),
            tiles.reshape(slots, width, width),
        )
        return pl.pallas_call(
            spell,
            out_shape=(
                jax.ShapeDtypeStruct((BR_DEV, 1, width), jnp.float32),
                jax.ShapeDtypeStruct((col_blocks, 1, width), jnp.float32),
            ),
            in_specs=[vmem, vmem],
            out_specs=(vmem, vmem),
        )(row_vec, col_vec)

    return jax.shard_map(
        on_device,
        mesh=mesh,
        in_specs=(
            P("prow", "pcol", None, None, None),
            P("prow", "pcol", None),
            P("prow", "pcol", None),
            P("prow", "pcol"),
        ),
        out_specs=(P(None, "prow", None), P(None, "pcol", None)),
        check_vma=False,
    )
```

profile of v0, /device:TPU:0, one launch (start us, length us, event | category | flops | bytes accessed | tf_op | source)
XLA Modules:
  0.0 30.9 jit_solution(15145041170249086329)
XLA Ops:
  1.3 28.2 %shard_map.59 = (f32[32,256]{1,0:T(8,128)}, f32[16,256]{1,0:T(8,128)}) custom-call(s32[32]{0:T(128)} %bitcast.6, s32[32]{0:T(128)} %bitcast.7, s32[1]{0:T(128)} %bitcast.4.count_ref, bf16[32,256,256]{2,1,0:T(8,128)(2,1)} %bitcast.5), custom_call_target="tpu_custom_call" | custom-call | tf_op jit(solution)/shard_map/pallas_call | solution.py:191
  29.5 1.4 %shard_map.60 = (f32[32,1,256]{2,1,0:T(1,128)}, f32[16,1,256]{2,1,0:T(1,128)}) custom-call(f32[32,256]{1,0:T(8,128)} %get-tuple-element.4.row_ref, f32[16,256]{1,0:T(8,128)} %get-tuple-element.5.col_ref), custom_call_target="tpu_custom_call" | custom-call | tf_op jit(solution)/shard_map/pallas_call | solution.py:226
where the time goes:
time: 31.1 us; the launch traced here: 30.9 us
  Pallas kernels  29.6 us (95%)
  between operations  1.29 us (4%)
    pallas_call x1, Pallas kernels, on_device(): pl.pallas_call(functools.partial(kernel, n_prow, n_pcol, col_blocks, slot...  28.2 us
    pallas_call x1, Pallas kernels, on_device(): pl.pallas_call(spell, out_shape=(jax.ShapeDtypeStruct((BR_DEV, 1, width),...  1.4 us

commit v1 on v0

--- a/solution.py
+++ b/solution.py
@@ -18,10 +18,19 @@
     return scale / jnp.sqrt(largest)
 
 
+def partner(at, mask, size):
+    out, bit = at, 1
+    while bit < size:
+        if mask & bit:
+            out = out + bit * (1 - 2 * lax.rem(lax.div(at, bit), 2))
+        bit *= 2
+    return out
+
+
 def kernel(
     n_prow, n_pcol, col_blocks, slots, width,
-    brow_ref, bcol_ref, count_ref, tiles_ref,
-    row_out, col_out,
+    brow_hbm, bcol_hbm, count_hbm, tiles_ref,
+    row_out, col_out, brow_ref, bcol_ref, count_ref, meta_sem,
     block, row_split, col_vec, spread_a, spread_b, peak_a, peak_b,
     row_send, part_recv, done_send, done_recv, col_send, col_recv,
     load_sem, part_send_sem, part_recv_sem,
@@ -33,6 +42,13 @@
 
     for t in range(slots // STEP):
         load(t).start()
+    metas = [
+        pltpu.make_async_copy(brow_hbm, brow_ref, meta_sem.at[0]),
+        pltpu.make_async_copy(bcol_hbm, bcol_ref, meta_sem.at[1]),
+        pltpu.make_async_copy(count_hbm, count_ref, meta_sem.at[2]),
+    ]
+    for m in metas:
+        m.start()
 
     pr = lax.axis_index("prow")
     pc = lax.axis_index("pcol")
@@ -42,6 +58,8 @@
     for d in range(1, n_prow):
         pl.semaphore_signal(barrier, inc=1, device_id={"prow": lax.rem(pr + d, n_prow)})
 
+    for m in metas:
+        m.wait()
     count = count_ref[0]
     row_ids = lax.broadcasted_iota(jnp.int32, (BR_DEV, width), 0)
     col_ids = lax.broadcasted_iota(jnp.int32, (col_blocks, width), 0)
@@ -131,8 +149,8 @@
         if sweep == 0:
             pl.semaphore_wait(barrier, n_pcol - 1 + n_prow - 1)
         part_copies = []
-        for d in range(1, n_pcol):
-            to = lax.rem(pc + d, n_pcol)
+        for d in range(n_pcol - 1, 0, -1):
+            to = partner(pc, d, n_pcol)
             part_copies.append(pltpu.make_async_remote_copy(
                 src_ref=row_send.at[sweep], dst_ref=part_recv.at[sweep, d - 1],
                 send_sem=part_send_sem.at[sweep, d - 1], recv_sem=part_recv_sem.at[sweep, d - 1],
@@ -155,7 +173,7 @@
         col_now = rescale(col_now, col_max)
         for d, copy in enumerate(part_copies):
             copy.wait()
-            row_max = jnp.maximum(row_max, part_recv[sweep, d])
+            row_max = jnp.maximum(row_max, part_recv[sweep, n_pcol - 2 - d])
         row_vec = rescale(row_vec, row_max)
         if sweep + 1 < SWEEPS:
             col_vec[...] = col_now
@@ -186,7 +204,7 @@
         slots, width = tiles.shape[2], tiles.shape[3]
         col_blocks = BR_DEV * n_prow // n_pcol
         share = BR_DEV // n_pcol
-        smem = pl.BlockSpec(memory_space=pltpu.SMEM)
+        anyb = pl.BlockSpec(memory_space=pl.ANY)
         vmem = pl.BlockSpec(memory_space=pltpu.VMEM)
         row_vec, col_vec = pl.pallas_call(
             functools.partial(kernel, n_prow, n_pcol, col_blocks, slots, width),
@@ -194,9 +212,10 @@
                 jax.ShapeDtypeStruct((BR_DEV, width), jnp.float32),
                 jax.ShapeDtypeStruct((col_blocks, width), jnp.float32),
             ),
-            in_specs=[smem, smem, smem, pl.BlockSpec(memory_space=pl.ANY)],
+            in_specs=[anyb, anyb, anyb, pl.BlockSpec(memory_space=pl.ANY)],
             out_specs=(vmem, vmem),
             scratch_shapes=[
+                pltpu.SMEM((slots,), jnp.int32), pltpu.SMEM((slots,), jnp.int32), pltpu.SMEM((1,), jnp.int32), pltpu.SemaphoreType.DMA((3,)),
                 pltpu.VMEM((slots, width, width), jnp.bfloat16),
                 pltpu.VMEM((width, LANES), jnp.bfloat16),
                 pltpu.VMEM((col_blocks, width), jnp.float32),
@@ -218,9 +237,9 @@
                 pltpu.SemaphoreType.DMA((SWEEPS, n_prow - 1)),
                 pltpu.SemaphoreType.DMA((SWEEPS, n_prow - 1)),
             ],
-            compiler_params=pltpu.CompilerParams(collective_id=0, has_side_effects=True),
+            compiler_params=pltpu.CompilerParams(collective_id=0, has_side_effects=True, vmem_limit_bytes=53 << 20),
         )(
-            tile_brow.reshape(slots), tile_bcol.reshape(slots), tile_count.reshape(1),
+            pltpu.with_memory_space_constraint(tile_brow.reshape(slots), pltpu.HBM), pltpu.with_memory_space_constraint(tile_bcol.reshape(slots), pltpu.HBM), tile_count.reshape(1),
             tiles.reshape(slots, width, width),
         )
         return pl.pallas_call(
@@ -231,6 +250,7 @@
             ),
             in_specs=[vmem, vmem],
             out_specs=(vmem, vmem),
+            compiler_params=pltpu.CompilerParams(vmem_limit_bytes=4 << 20),
         )(row_vec, col_vec)
 
     return jax.shard_map(

time: 31.1 us -> 29.5 us (0.949)
  Pallas kernels: 29.6 us -> 28 us
    pallas_call x1, Pallas kernels: 28.2 us -> 27.4 us  [on_device(): pl.pallas_call(functools.partial(kernel, n_prow, n_pcol, col_blocks, slot...]
    pallas_call x1, Pallas kernels: 1.4 us -> 0.64 us  [on_device(): pl.pallas_call(spell, out_shape=(jax.ShapeDtypeStruct((BR_DEV, 1, width),...]
where the time goes in v1:
time: 29.5 us; the launch traced here: 29.3 us
  Pallas kernels  28 us (95%)
  between operations  1.29 us (4%)
    pallas_call x1, Pallas kernels, on_device(): pl.pallas_call(functools.partial(kernel, n_prow, n_pcol, col_blocks, slot...  27.4 us
    pallas_call x1, Pallas kernels, on_device(): pl.pallas_call(spell, out_shape=(jax.ShapeDtypeStruct((BR_DEV, 1, width),...  0.64 us

profile of v1, /device:TPU:0, one launch (start us, length us, event | category | flops | bytes accessed | tf_op | source)
XLA Modules:
  0.0 29.3 jit_solution(11649555665401389838)
XLA Ops:
  1.3 27.4 %shard_map.59 = (f32[32,256]{1,0:T(8,128)S(1)}, f32[16,256]{1,0:T(8,128)S(1)}) custom-call(s32[32]{0:T(128)} %bitcast.6, s32[32]{0:T(128)} %bitcast.7, s32[1]{0:T(128)} %bitcast.4.count_hbm, bf16[32,256,256]{2,1,0:T(8,128)(2,1)} %bitcast.5), custom_call_target="tpu_custom_call" | custom-call | tf_op jit(solution)/shard_map/pallas_call | solution.py:209
  28.7 0.6 %shard_map.60 = (f32[32,1,256]{2,1,0:T(1,128)}, f32[16,1,256]{2,1,0:T(1,128)}) custom-call(f32[32,256]{1,0:T(8,128)S(1)} %get-tuple-element.4.row_ref, f32[16,256]{1,0:T(8,128)S(1)} %get-tuple-element.5.col_ref), custom_call_target="tpu_custom_call" | custom-call | tf_op jit(solution)/shard_map/pallas_call | solution.py:245

commit v2 on v1

v2 whole, which is shorter than its diff:
```python
import functools
import math

import jax
import jax.numpy as jnp
from jax import lax
from jax.experimental import pallas as pl
from jax.experimental.pallas import tpu as pltpu
from jax.sharding import PartitionSpec as P

BR_DEV = 32
SWEEPS = 3
LANES = 128
SUB = 8
STEP = 4
PACK = 16
LIFT = 2.0 ** 63


def rescale(scale, largest):
    return scale / jnp.sqrt(largest)


def partner(at, mask, size):
    out, bit = at, 1
    while bit < size:
        if mask & bit:
            out = out + bit * (1 - 2 * lax.rem(lax.div(at, bit), 2))
        bit *= 2
    return out


def kernel(
    n_prow, n_pcol, col_blocks, slots, width,
    brow_hbm, bcol_hbm, count_hbm, tiles_ref,
    row_out, col_out,
    brow_ref, bcol_ref, count_ref,
    block, plain, turned, row_slot, col_slot, split, spread_a, spread_b, col_vec,
    ids, row_buf, col_buf,
    meta_sem, load_sem, ids_send_sem, ids_recv_sem,
    row_send_sem, row_recv_sem, col_send_sem, col_recv_sem,
):
    halves = width // LANES
    group = math.gcd(n_prow, n_pcol)
    few = slots // 2
    pr = lax.axis_index("prow")
    pc = lax.axis_index("pcol")
    holder = lax.rem(pc, group) == lax.rem(pr, group)
    steps = jnp.where(holder, slots, few) // STEP

    def load(t):
        at = pl.ds(t * STEP, STEP)
        return pltpu.make_async_copy(tiles_ref.at[at], block.at[at], load_sem.at[t])

    for t in range(few // STEP):
        load(t).start()

    @pl.when(holder)
    def _():
        for t in range(few // STEP, slots // STEP):
            load(t).start()

    metas = [
        pltpu.make_async_copy(brow_hbm, brow_ref, meta_sem.at[0]),
        pltpu.make_async_copy(bcol_hbm, bcol_ref, meta_sem.at[1]),
        pltpu.make_async_copy(count_hbm, count_ref, meta_sem.at[2]),
    ]
    for meta in metas:
        meta.start()
    barrier = pltpu.get_barrier_semaphore()
    for m in range(1, n_pcol):
        pl.semaphore_signal(barrier, inc=1, device_id={"pcol": partner(pc, m, n_pcol)})
    for m in range(1, n_prow):
        pl.semaphore_signal(barrier, inc=1, device_id={"prow": partner(pr, m, n_prow)})

    row_ids = lax.broadcasted_iota(jnp.int32, (BR_DEV, LANES), 0)
    col_ids = lax.broadcasted_iota(jnp.int32, (col_blocks, LANES), 0)
    pick_row = lax.broadcasted_iota(jnp.int32, (LANES, 2 * LANES), 0)
    pick_lane = lax.broadcasted_iota(jnp.int32, (1, 2 * LANES), 1)

    def lanes(h):
        return slice(h * LANES, (h + 1) * LANES)

    def widest(parts):
        while len(parts) > 1:
            pairs = [jnp.maximum(a, b) for a, b in zip(parts[::2], parts[1::2])]
            parts = pairs + parts[len(parts) - len(parts) % 2:]
        return parts[0]

    def keep(ref, s, h, top):
        ref[h, pl.ds(pl.multiple_of(s * SUB, SUB), SUB), :] = top

    def tops(ref, h, n):
        return widest([ref[h, pl.ds(k, n, stride=SUB), :] for k in range(SUB)])

    def first_tile(s):
        x = [[jnp.abs(block[s, g * PACK:(g + 1) * PACK, lanes(h)]) for h in range(halves)]
             for g in range(width // PACK)]
        for h in range(halves):
            top = widest([row[h] for row in x]).astype(jnp.float32)
            keep(col_slot, s, h, jnp.maximum(top[:SUB], top[SUB:]))
        fold = jnp.concatenate([widest(row) for row in x], axis=0).T
        top = widest([fold[k * PACK:(k + 1) * PACK] for k in range(LANES // PACK)])
        top = top.astype(jnp.float32)
        top = jnp.maximum(top[:SUB], top[SUB:])
        for h in range(halves):
            keep(row_slot, s, h, top[:, lanes(h)])

    def first_step(t, carry):
        load(t).wait()
        for j in range(STEP):
            first_tile(t * STEP + j)
        return carry

    def prepare(s, carry):
        x = jnp.abs(block[s])
        plain[s] = x.astype(jnp.float32)
        turned[s] = x.T.astype(jnp.float32)
        return carry

    def set_split(vec):
        n = vec.shape[0]
        top = vec.astype(jnp.bfloat16)
        left = vec - top.astype(jnp.float32)
        mid = left.astype(jnp.bfloat16)
        low = (left - mid.astype(jnp.float32)).astype(jnp.bfloat16)
        rest = jnp.zeros((LANES - 3 * n, width), jnp.bfloat16)
        stack = jnp.concatenate([top, mid, low, rest], axis=0)
        for h in range(halves):
            split[lanes(h), :] = stack[:, lanes(h)].T

    def spread_pair(ids_ref, n, s, out):
        a = ids_ref[jnp.minimum(s, slots - 1)]
        b = ids_ref[jnp.minimum(s + 1, slots - 1)]
        want = jnp.where(pick_lane < LANES, a, b)
        hit = (pick_row == want) | (pick_row == want + n) | (pick_row == want + 2 * n)
        pick = jnp.where(hit, 1.0, 0.0).astype(jnp.bfloat16)
        out[...] = jnp.dot(split[...], pick, preferred_element_type=jnp.float32)

    def scale_tile(data, s, j, spread, slot, store):
        best = [[None, None] for _ in range(halves)]
        for g in range(width // SUB):
            at = slice(g * SUB, (g + 1) * SUB)
            by = spread[at, lanes(j)]
            for h in range(halves):
                x = data[s, at, lanes(h)] * by
                if store:
                    data[s, at, lanes(h)] = x
                old = best[h][g % 2]
                best[h][g % 2] = x if old is None else jnp.maximum(old, x)
        for h in range(halves):
            keep(slot, s, h, jnp.maximum(*best[h]))

    def one_pass(data, vec, ids_ref, slot, store):
        set_split(vec)
        n = vec.shape[0]
        spread_pair(ids_ref, n, 0, spread_a)

        def body(t, carry):
            s = t * STEP
            spread_pair(ids_ref, n, s + 2, spread_b)
            for j in range(2):
                scale_tile(data, s + j, j, spread_a, slot, store)
            spread_pair(ids_ref, n, s + 4, spread_a)
            for j in range(2):
                scale_tile(data, s + 2 + j, j, spread_b, slot, store)
            return carry

        lax.fori_loop(0, steps, body, 0)

    def live_id(ref, s):
        return jnp.where(s < count_ref[0], ref[s], -1)

    def gather_slots(ref, ids_ref, where_ids, n, out):
        for h in range(halves):
            top = tops(ref, h, n)
            acc = jnp.zeros(where_ids.shape, jnp.float32)
            for s in range(n):
                acc = jnp.maximum(
                    acc, jnp.where(where_ids == live_id(ids_ref, s), top[s:s + 1, :], 0.0)
                )
            out[:, lanes(h)] = acc

    def row_copies(k, rows):
        return [pltpu.make_async_remote_copy(
            src_ref=row_buf.at[k, pc, pl.ds(0, rows)], dst_ref=row_buf.at[k, pc, pl.ds(0, rows)],
            send_sem=row_send_sem.at[k, m - 1], recv_sem=row_recv_sem.at[k, pc],
            device_id={"pcol": partner(pc, m, n_pcol)},
        ) for m in range(n_pcol - 1, 0, -1)]

    def ids_copies():
        return [pltpu.make_async_remote_copy(
            src_ref=ids.at[pc], dst_ref=ids.at[pc],
            send_sem=ids_send_sem.at[m - 1], recv_sem=ids_recv_sem.at[pc],
            device_id={"pcol": partner(pc, m, n_pcol)},
        ) for m in range(n_pcol - 1, 0, -1)]

    def col_copies(k):
        return [pltpu.make_async_remote_copy(
            src_ref=col_buf.at[k, pr], dst_ref=col_buf.at[k, pr],
            send_sem=col_send_sem.at[k, m - 1], recv_sem=col_recv_sem.at[k, pr],
            device_id={"prow": partner(pr, m, n_prow)},
        ) for m in range(n_prow - 1, 0, -1)]

    def send_rows(k):
        @pl.when(holder)
        def _():
            gather_slots(row_slot, brow_ref, row_ids, slots, row_buf.at[k, pc])
            for copy in row_copies(k, BR_DEV):
                copy.start()

        @pl.when(jnp.logical_not(holder))
        def _():
            for h in range(halves):
                row_buf[k, pc, :few, lanes(h)] = tops(row_slot, h, few)
            for copy in row_copies(k, few):
                copy.start()

    def send_cols(k):
        @pl.when(holder)
        def _():
            gather_slots(col_slot, bcol_ref, col_ids, slots, col_buf.at[k, pr])

        @pl.when(jnp.logical_not(holder))
        def _():
            gather_slots(col_slot, bcol_ref, col_ids, few, col_buf.at[k, pr])

        for copy in col_copies(k):
            copy.start()

    def arrived(copy):
        copy.wait_recv()

    def wait_rows(k):
        per = n_pcol // group

        def from_few(i, acc):
            q = lax.rem(lax.rem(pr, group) + 1 + lax.div(i, per), group) + group * lax.rem(i, per)

            @pl.when(q != pc)
            def _():
                ref = row_buf.at[k, q, pl.ds(0, few)]
                pltpu.make_async_remote_copy(
                    src_ref=ref, dst_ref=ref, send_sem=row_send_sem.at[k, 0],
                    recv_sem=row_recv_sem.at[k, q], device_id={"pcol": q},
                ).wait_recv()
                if k == 0:
                    pltpu.make_async_remote_copy(
                        src_ref=ids.at[q], dst_ref=ids.at[q], send_sem=ids_send_sem.at[0],
                        recv_sem=ids_recv_sem.at[q], device_id={"pcol": q},
                    ).wait_recv()

            acc = list(acc)
            for s in range(few):
                hit = row_ids == ids[q, s:s + 1, :]
                for h in range(halves):
                    top = row_buf[k, q, s:s + 1, lanes(h)]
                    acc[h] = jnp.maximum(acc[h], jnp.where(hit, top, 0.0))
            return tuple(acc)

        acc = lax.fori_loop(
            0, n_pcol - per, from_few,
            tuple(jnp.zeros((BR_DEV, LANES), jnp.float32) for _ in range(halves)),
        )
        acc = jnp.concatenate(acc, axis=1)
        for i in range(per):
            q = lax.rem(pr, group) + group * i

            @pl.when(q != pc)
            def _():
                ref = row_buf.at[k, q]
                pltpu.make_async_remote_copy(
                    src_ref=ref, dst_ref=ref, send_sem=row_send_sem.at[k, 0],
                    recv_sem=row_recv_sem.at[k, q], device_id={"pcol": q},
                ).wait_recv()

            acc = jnp.maximum(acc, row_buf[k, q])
        return acc

    def wait_cols(k):
        for m in range(n_prow - 1, 0, -1):
            q = partner(pr, m, n_prow)
            ref = col_buf.at[k, q]
            pltpu.make_async_remote_copy(
                src_ref=ref, dst_ref=ref, send_sem=col_send_sem.at[k, m - 1],
                recv_sem=col_recv_sem.at[k, q], device_id={"prow": q},
            ).wait_recv()
        return widest([col_buf[k, q] for q in range(n_prow)])

    lax.fori_loop(0, steps, first_step, 0)
    for meta in metas:
        meta.wait()
    pl.semaphore_wait(barrier, n_pcol - 1 + n_prow - 1)
    send_rows(0)
    send_cols(0)

    @pl.when(jnp.logical_not(holder))
    def _():
        for s in range(few):
            ids[pc, s:s + 1, :] = jnp.full((1, LANES), live_id(brow_ref, s), jnp.int32)
        for copy in ids_copies():
            copy.start()

    lax.fori_loop(0, steps * STEP, prepare, 0)

    one = jnp.ones((BR_DEV, width), jnp.float32)
    row_1 = rescale(one, wait_rows(0))
    one_pass(plain, row_1, brow_ref, col_slot, False)
    send_cols(1)
    col_1 = rescale(jnp.ones((col_blocks, width), jnp.float32), wait_cols(0))
    lifted = col_1 * LIFT
    one_pass(turned, lifted, bcol_ref, row_slot, True)
    send_rows(1)
    col_vec[...] = lifted

    def lift_plain(s, carry):
        by = col_vec[pl.ds(bcol_ref[s], 1), :]
        plain[s] = plain[s] * by
        return carry

    lax.fori_loop(0, steps * STEP, lift_plain, 0)
    col_max = col_1 * wait_cols(1)
    col_2 = rescale(col_1, col_max)
    change = 1.0 / jnp.sqrt(col_max)
    one_pass(turned, change, bcol_ref, row_slot, False)
    send_rows(2)
    row_2 = rescale(row_1, (row_1 * wait_rows(1)) / LIFT)
    one_pass(plain, row_2, brow_ref, col_slot, False)
    send_cols(2)
    row_out[...] = rescale(row_2, (row_2 * wait_rows(2)) / LIFT)
    col_out[...] = rescale(col_2, (change * wait_cols(2)) / LIFT)

    for k in range(SWEEPS):
        @pl.when(holder)
        def _():
            for copy in row_copies(k, BR_DEV):
                copy.wait_send()

        @pl.when(jnp.logical_not(holder))
        def _():
            for copy in row_copies(k, few):
                copy.wait_send()
            if k == 0:
                for copy in ids_copies():
                    copy.wait_send()

        for copy in col_copies(k):
            copy.wait_send()


def spell(row_ref, col_ref, row_out, col_out):
    for ref, out in ((row_ref, row_out), (col_ref, col_out)):
        for i in range(ref.shape[0]):
            out[i] = ref[i:i + 1, :]


def solution(mesh):
    n_prow, n_pcol = mesh.shape["prow"], mesh.shape["pcol"]

    def on_device(tiles, tile_brow, tile_bcol, tile_count):
        slots, width = tiles.shape[2], tiles.shape[3]
        col_blocks = BR_DEV * n_prow // n_pcol
        halves = width // LANES
        vmem = pl.BlockSpec(memory_space=pltpu.VMEM)
        anywhere = pl.BlockSpec(memory_space=pl.ANY)
        row_vec, col_vec = pl.pallas_call(
            functools.partial(kernel, n_prow, n_pcol, col_blocks, slots, width),
            out_shape=(
                jax.ShapeDtypeStruct((BR_DEV, width), jnp.float32),
                jax.ShapeDtypeStruct((col_blocks, width), jnp.float32),
            ),
            in_specs=[anywhere] * 4,
            out_specs=(vmem, vmem),
            scratch_shapes=[
                pltpu.SMEM((slots,), jnp.int32),
                pltpu.SMEM((slots,), jnp.int32),
                pltpu.SMEM((1,), jnp.int32),
                pltpu.VMEM((slots, width, width), jnp.bfloat16),
                pltpu.VMEM((slots, width, width), jnp.float32),
                pltpu.VMEM((slots, width, width), jnp.float32),
                pltpu.VMEM((halves, slots * SUB, LANES), jnp.float32),
                pltpu.VMEM((halves, slots * SUB, LANES), jnp.float32),
                pltpu.VMEM((width, LANES), jnp.bfloat16),
                pltpu.VMEM((width, 2 * LANES), jnp.float32),
                pltpu.VMEM((width, 2 * LANES), jnp.float32),
                pltpu.VMEM((col_blocks, width), jnp.float32),
                pltpu.VMEM((n_pcol, slots // 2, LANES), jnp.int32),
                pltpu.VMEM((SWEEPS, n_pcol, BR_DEV, width), jnp.float32),
                pltpu.VMEM((SWEEPS, n_prow, col_blocks, width), jnp.float32),
                pltpu.SemaphoreType.DMA((3,)),
                pltpu.SemaphoreType.DMA((slots // STEP,)),
                pltpu.SemaphoreType.DMA((n_pcol - 1,)),
                pltpu.SemaphoreType.DMA((n_pcol,)),
                pltpu.SemaphoreType.DMA((SWEEPS, n_pcol - 1)),
                pltpu.SemaphoreType.DMA((SWEEPS, n_pcol)),
                pltpu.SemaphoreType.DMA((SWEEPS, n_prow - 1)),
                pltpu.SemaphoreType.DMA((SWEEPS, n_prow)),
            ],
            compiler_params=pltpu.CompilerParams(
                collective_id=0, has_side_effects=True, vmem_limit_bytes=53 << 20
            ),
        )(
            pltpu.with_memory_space_constraint(tile_brow.reshape(slots), pltpu.HBM),
            pltpu.with_memory_space_constraint(tile_bcol.reshape(slots), pltpu.HBM),
            tile_count.reshape(1),
            tiles.reshape(slots, width, width),
        )
        return pl.pallas_call(
            spell,
            out_shape=(
                jax.ShapeDtypeStruct((BR_DEV, 1, width), jnp.float32),
                jax.ShapeDtypeStruct((col_blocks, 1, width), jnp.float32),
            ),
            in_specs=[vmem, vmem],
            out_specs=(vmem, vmem),
            compiler_params=pltpu.CompilerParams(vmem_limit_bytes=4 << 20),
        )(row_vec, col_vec)

    return jax.shard_map(
        on_device,
        mesh=mesh,
        in_specs=(
            P("prow", "pcol", None, None, None),
            P("prow", "pcol", None),
            P("prow", "pcol", None),
            P("prow", "pcol"),
        ),
        out_specs=(P(None, "prow", None), P(None, "pcol", None)),
        check_vma=False,
    )
```

time: 29.5 us -> 27.3 us (0.925)
  Pallas kernels: 28 us -> 25.8 us
    pallas_call x1, Pallas kernels: 27.4 us -> 25.2 us  [on_device(): pl.pallas_call(functools.partial(kernel, n_prow, n_pcol, col_blocks, slot...]
where the time goes in v2:
time: 27.3 us; the launch traced here: 27.1 us
  Pallas kernels  25.8 us (95%)
  between operations  1.29 us (5%)
    pallas_call x1, Pallas kernels, on_device(): pl.pallas_call(functools.partial(kernel, n_prow, n_pcol, col_blocks, slot...  25.2 us
    pallas_call x1, Pallas kernels, on_device(): pl.pallas_call(spell, out_shape=(jax.ShapeDtypeStruct((BR_DEV, 1, width),...  0.64 us

profile of v2, /device:TPU:0, one launch (start us, length us, event | category | flops | bytes accessed | tf_op | source)
XLA Modules:
  0.0 27.1 jit_solution(4029263620711333340)
XLA Ops:
  1.3 25.2 %shard_map.59 = (f32[32,256]{1,0:T(8,128)S(1)}, f32[16,256]{1,0:T(8,128)S(1)}) custom-call(s32[32]{0:T(128)} %bitcast.6, s32[32]{0:T(128)} %bitcast.7, s32[1]{0:T(128)} %bitcast.4.count_hbm, bf16[32,256,256]{2,1,0:T(8,128)(2,1)} %bitcast.5), custom_call_target="tpu_custom_call" | custom-call | tf_op jit(solution)/shard_map/pallas_call | solution.py:366
  26.5 0.6 %shard_map.60 = (f32[32,1,256]{2,1,0:T(1,128)}, f32[16,1,256]{2,1,0:T(1,128)}) custom-call(f32[32,256]{1,0:T(8,128)S(1)} %get-tuple-element.4.row_ref, f32[16,256]{1,0:T(8,128)S(1)} %get-tuple-element.5.col_ref), custom_call_target="tpu_custom_call" | custom-call | tf_op jit(solution)/shard_map/pallas_call | solution.py:408

commit v3 on v2

--- a/solution.py
+++ b/solution.py
@@ -35,7 +35,7 @@
     brow_hbm, bcol_hbm, count_hbm, tiles_ref,
     row_out, col_out,
     brow_ref, bcol_ref, count_ref,
-    block, plain, turned, row_slot, col_slot, split, spread_a, spread_b, col_vec,
+    block, plain, turned, row_slot, col_slot, split, spread, row_table, col_table, row_vec, slot_top, own_ids,
     ids, row_buf, col_buf,
     meta_sem, load_sem, ids_send_sem, ids_recv_sem,
     row_send_sem, row_recv_sem, col_send_sem, col_recv_sem,
@@ -75,8 +75,12 @@
 
     row_ids = lax.broadcasted_iota(jnp.int32, (BR_DEV, LANES), 0)
     col_ids = lax.broadcasted_iota(jnp.int32, (col_blocks, LANES), 0)
-    pick_row = lax.broadcasted_iota(jnp.int32, (LANES, 2 * LANES), 0)
-    pick_lane = lax.broadcasted_iota(jnp.int32, (1, 2 * LANES), 1)
+    line = lax.broadcasted_iota(jnp.int32, (LANES, LANES), 0)
+    for table, n in ((row_table, BR_DEV), (col_table, col_blocks)):
+        turn = jnp.where(line < 3 * n, lax.rem(line, n), -2)
+        turn = turn.astype(jnp.float32).astype(jnp.bfloat16)
+        for i in range(n):
+            table[i] = jnp.maximum(1.0 - jnp.abs(turn - float(i)), 0.0).astype(jnp.bfloat16)
 
     def lanes(h):
         return slice(h * LANES, (h + 1) * LANES)
@@ -129,57 +133,51 @@
         for h in range(halves):
             split[lanes(h), :] = stack[:, lanes(h)].T
 
-    def spread_pair(ids_ref, n, s, out):
-        a = ids_ref[jnp.minimum(s, slots - 1)]
-        b = ids_ref[jnp.minimum(s + 1, slots - 1)]
-        want = jnp.where(pick_lane < LANES, a, b)
-        hit = (pick_row == want) | (pick_row == want + n) | (pick_row == want + 2 * n)
-        pick = jnp.where(hit, 1.0, 0.0).astype(jnp.bfloat16)
-        out[...] = jnp.dot(split[...], pick, preferred_element_type=jnp.float32)
-
-    def scale_tile(data, s, j, spread, slot, store):
+    def spread_pair(ids_ref, table, p):
+        pick = jnp.concatenate([table[ids_ref[2 * p + j]] for j in range(2)], axis=1)
+        spread[p] = jnp.dot(split[...], pick, preferred_element_type=jnp.float32)
+
+    def scale_tile(data, s, slot):
         best = [[None, None] for _ in range(halves)]
         for g in range(width // SUB):
             at = slice(g * SUB, (g + 1) * SUB)
-            by = spread[at, lanes(j)]
+            by = spread[s // 2, at, lanes(s % 2)]
             for h in range(halves):
                 x = data[s, at, lanes(h)] * by
-                if store:
-                    data[s, at, lanes(h)] = x
                 old = best[h][g % 2]
                 best[h][g % 2] = x if old is None else jnp.maximum(old, x)
         for h in range(halves):
             keep(slot, s, h, jnp.maximum(*best[h]))
 
-    def one_pass(data, vec, ids_ref, slot, store):
+    def one_pass(data, vec, ids_ref, slot):
         set_split(vec)
-        n = vec.shape[0]
-        spread_pair(ids_ref, n, 0, spread_a)
-
-        def body(t, carry):
-            s = t * STEP
-            spread_pair(ids_ref, n, s + 2, spread_b)
-            for j in range(2):
-                scale_tile(data, s + j, j, spread_a, slot, store)
-            spread_pair(ids_ref, n, s + 4, spread_a)
-            for j in range(2):
-                scale_tile(data, s + 2 + j, j, spread_b, slot, store)
-            return carry
-
-        lax.fori_loop(0, steps, body, 0)
-
-    def live_id(ref, s):
-        return jnp.where(s < count_ref[0], ref[s], -1)
-
-    def gather_slots(ref, ids_ref, where_ids, n, out):
-        for h in range(halves):
-            top = tops(ref, h, n)
-            acc = jnp.zeros(where_ids.shape, jnp.float32)
-            for s in range(n):
-                acc = jnp.maximum(
-                    acc, jnp.where(where_ids == live_id(ids_ref, s), top[s:s + 1, :], 0.0)
-                )
-            out[:, lanes(h)] = acc
+        table = row_table if ids_ref is brow_ref else col_table
+        half, pairs = few // 2, slots // 2
+        ahead = half + half // 2
+        for p in range(ahead):
+            spread_pair(ids_ref, table, p)
+            if 2 <= p < half + 2:
+                for j in range(2):
+                    scale_tile(data, 2 * (p - 2) + j, slot)
+
+        @pl.when(holder)
+        def _():
+            for p in range(ahead, pairs):
+                spread_pair(ids_ref, table, p)
+            for s in range(few, slots):
+                scale_tile(data, s, slot)
+
+    def gather_slots(ref, kind, where_ids, n, out):
+        for h in range(halves):
+            slot_top[:n, lanes(h)] = tops(ref, h, n)
+        acc = [jnp.zeros(where_ids.shape, jnp.float32) for _ in range(halves)]
+        for s in range(n):
+            hit = where_ids == own_ids[kind, s:s + 1, :]
+            for h in range(halves):
+                top = slot_top[s:s + 1, lanes(h)]
+                acc[h] = jnp.maximum(acc[h], jnp.where(hit, top, 0.0))
+        for h in range(halves):
+            out[:, lanes(h)] = acc[h]
 
     def row_copies(k, rows):
         return [pltpu.make_async_remote_copy(
@@ -205,7 +203,7 @@
     def send_rows(k):
         @pl.when(holder)
         def _():
-            gather_slots(row_slot, brow_ref, row_ids, slots, row_buf.at[k, pc])
+            gather_slots(row_slot, 1, row_ids, slots, row_buf.at[k, pc])
             for copy in row_copies(k, BR_DEV):
                 copy.start()
 
@@ -219,11 +217,11 @@
     def send_cols(k):
         @pl.when(holder)
         def _():
-            gather_slots(col_slot, bcol_ref, col_ids, slots, col_buf.at[k, pr])
+            gather_slots(col_slot, 0, col_ids, slots, col_buf.at[k, pr])
 
         @pl.when(jnp.logical_not(holder))
         def _():
-            gather_slots(col_slot, bcol_ref, col_ids, few, col_buf.at[k, pr])
+            gather_slots(col_slot, 0, col_ids, few, col_buf.at[k, pr])
 
         for copy in col_copies(k):
             copy.start()
@@ -234,8 +232,11 @@
     def wait_rows(k):
         per = n_pcol // group
 
-        def from_few(i, acc):
-            q = lax.rem(lax.rem(pr, group) + 1 + lax.div(i, per), group) + group * lax.rem(i, per)
+        def place(i):
+            return lax.rem(lax.rem(pr, group) + 1 + lax.div(i, per), group) + group * lax.rem(i, per)
+
+        def wait_few(i):
+            q = place(i)
 
             @pl.when(q != pc)
             def _():
@@ -250,18 +251,24 @@
                         recv_sem=ids_recv_sem.at[q], device_id={"pcol": q},
                     ).wait_recv()
 
+        def from_few(first, n, acc):
+            for i in range(n):
+                wait_few(first + i)
             acc = list(acc)
-            for s in range(few):
-                hit = row_ids == ids[q, s:s + 1, :]
-                for h in range(halves):
-                    top = row_buf[k, q, s:s + 1, lanes(h)]
-                    acc[h] = jnp.maximum(acc[h], jnp.where(hit, top, 0.0))
+            for i in range(n):
+                q = place(first + i)
+                for s in range(few):
+                    hit = row_ids == ids[q, s:s + 1, :]
+                    for h in range(halves):
+                        top = row_buf[k, q, s:s + 1, lanes(h)]
+                        acc[h] = jnp.maximum(acc[h], jnp.where(hit, top, 0.0))
             return tuple(acc)
 
+        zero = tuple(jnp.zeros((BR_DEV, LANES), jnp.float32) for _ in range(halves))
+        rest, span = n_pcol - per, 3
         acc = lax.fori_loop(
-            0, n_pcol - per, from_few,
-            tuple(jnp.zeros((BR_DEV, LANES), jnp.float32) for _ in range(halves)),
-        )
+            0, rest // span, lambda i, acc: from_few(i * span, span, acc), zero
+        ) if rest > 2 * span else from_few(0, rest, zero)
         acc = jnp.concatenate(acc, axis=1)
         for i in range(per):
             q = lax.rem(pr, group) + group * i
@@ -287,17 +294,20 @@
             ).wait_recv()
         return widest([col_buf[k, q] for q in range(n_prow)])
 
-    lax.fori_loop(0, steps, first_step, 0)
     for meta in metas:
         meta.wait()
+    for kind, ref in enumerate((bcol_ref, brow_ref)):
+        for s in range(slots):
+            own = jnp.where(s < count_ref[0], ref[s], -1)
+            own_ids[kind, s:s + 1, :] = jnp.full((1, LANES), own, jnp.int32)
+    ids[pc] = own_ids[1, :few]
+    lax.fori_loop(0, steps, first_step, 0)
     pl.semaphore_wait(barrier, n_pcol - 1 + n_prow - 1)
     send_rows(0)
     send_cols(0)
 
     @pl.when(jnp.logical_not(holder))
     def _():
-        for s in range(few):
-            ids[pc, s:s + 1, :] = jnp.full((1, LANES), live_id(brow_ref, s), jnp.int32)
         for copy in ids_copies():
             copy.start()
 
@@ -305,30 +315,28 @@
 
     one = jnp.ones((BR_DEV, width), jnp.float32)
     row_1 = rescale(one, wait_rows(0))
-    one_pass(plain, row_1, brow_ref, col_slot, False)
+    one_pass(plain, row_1, brow_ref, col_slot)
     send_cols(1)
     col_1 = rescale(jnp.ones((col_blocks, width), jnp.float32), wait_cols(0))
-    lifted = col_1 * LIFT
-    one_pass(turned, lifted, bcol_ref, row_slot, True)
+    one_pass(turned, col_1 * LIFT, bcol_ref, row_slot)
     send_rows(1)
-    col_vec[...] = lifted
-
-    def lift_plain(s, carry):
-        by = col_vec[pl.ds(bcol_ref[s], 1), :]
-        plain[s] = plain[s] * by
+    row_vec[...] = row_1
+
+    def scale_turned(s, carry):
+        turned[s] = turned[s] * row_vec[pl.ds(brow_ref[s], 1), :]
         return carry
 
-    lax.fori_loop(0, steps * STEP, lift_plain, 0)
-    col_max = col_1 * wait_cols(1)
-    col_2 = rescale(col_1, col_max)
-    change = 1.0 / jnp.sqrt(col_max)
-    one_pass(turned, change, bcol_ref, row_slot, False)
+    lax.fori_loop(0, steps * STEP, scale_turned, 0)
+    col_2 = rescale(col_1, col_1 * wait_cols(1))
+    one_pass(turned, col_2, bcol_ref, row_slot)
     send_rows(2)
-    row_2 = rescale(row_1, (row_1 * wait_rows(1)) / LIFT)
-    one_pass(plain, row_2, brow_ref, col_slot, False)
+    row_max = (row_1 * wait_rows(1)) / LIFT
+    row_2 = rescale(row_1, row_max)
+    one_pass(plain, row_2, brow_ref, col_slot)
     send_cols(2)
-    row_out[...] = rescale(row_2, (row_2 * wait_rows(2)) / LIFT)
-    col_out[...] = rescale(col_2, (change * wait_cols(2)) / LIFT)
+    change = 1.0 / jnp.sqrt(row_max)
+    row_out[...] = rescale(row_2, change * wait_rows(2))
+    col_out[...] = rescale(col_2, col_2 * wait_cols(2))
 
     for k in range(SWEEPS):
         @pl.when(holder)
@@ -381,9 +389,12 @@
                 pltpu.VMEM((halves, slots * SUB, LANES), jnp.float32),
                 pltpu.VMEM((halves, slots * SUB, LANES), jnp.float32),
                 pltpu.VMEM((width, LANES), jnp.bfloat16),
-                pltpu.VMEM((width, 2 * LANES), jnp.float32),
-                pltpu.VMEM((width, 2 * LANES), jnp.float32),
-                pltpu.VMEM((col_blocks, width), jnp.float32),
+                pltpu.VMEM((slots // 2, width, 2 * LANES), jnp.float32),
+                pltpu.VMEM((BR_DEV, LANES, LANES), jnp.bfloat16),
+                pltpu.VMEM((col_blocks, LANES, LANES), jnp.bfloat16),
+                pltpu.VMEM((BR_DEV, width), jnp.float32),
+                pltpu.VMEM((slots, width), jnp.float32),
+                pltpu.VMEM((2, slots, LANES), jnp.int32),
                 pltpu.VMEM((n_pcol, slots // 2, LANES), jnp.int32),
                 pltpu.VMEM((SWEEPS, n_pcol, BR_DEV, width), jnp.float32),
                 pltpu.VMEM((SWEEPS, n_prow, col_blocks, width), jnp.float32),

time: 27.3 us -> 23.5 us (0.86)
  Pallas kernels: 25.8 us -> 22.1 us
    pallas_call x1, Pallas kernels: 25.2 us -> 21.5 us  [on_device(): pl.pallas_call(functools.partial(kernel, n_prow, n_pcol, col_blocks, slot...]
where the time goes in v3:
time: 23.5 us; the launch traced here: 23.4 us
  Pallas kernels  22.1 us (94%)
  between operations  1.29 us (5%)
    pallas_call x1, Pallas kernels, on_device(): pl.pallas_call(functools.partial(kernel, n_prow, n_pcol, col_blocks, slot...  21.5 us
    pallas_call x1, Pallas kernels, on_device(): pl.pallas_call(spell, out_shape=(jax.ShapeDtypeStruct((BR_DEV, 1, width),...  0.64 us

profile of v3, /device:TPU:0, one launch (start us, length us, event | category | flops | bytes accessed | tf_op | source)
XLA Modules:
  0.0 23.4 jit_solution(4934835290300644475)
XLA Ops:
  1.3 21.5 %shard_map.59 = (f32[32,256]{1,0:T(8,128)S(1)}, f32[16,256]{1,0:T(8,128)S(1)}) custom-call(s32[32]{0:T(128)} %bitcast.6, s32[32]{0:T(128)} %bitcast.7, s32[1]{0:T(128)} %bitcast.4.count_hbm, bf16[32,256,256]{2,1,0:T(8,128)(2,1)} %bitcast.5), custom_call_target="tpu_custom_call" | custom-call | tf_op jit(solution)/shard_map/pallas_call | solution.py:374
  22.7 0.6 %shard_map.60 = (f32[32,1,256]{2,1,0:T(1,128)}, f32[16,1,256]{2,1,0:T(1,128)}) custom-call(f32[32,256]{1,0:T(8,128)S(1)} %get-tuple-element.4.row_ref, f32[16,256]{1,0:T(8,128)S(1)} %get-tuple-element.5.col_ref), custom_call_target="tpu_custom_call" | custom-call | tf_op jit(solution)/shard_map/pallas_call | solution.py:419

commit v4 on v3

--- a/solution.py
+++ b/solution.py
@@ -14,6 +14,7 @@
 SUB = 8
 STEP = 4
 PACK = 16
+LEAD = 2
 LIFT = 2.0 ** 63
 
 
@@ -36,7 +37,7 @@
     row_out, col_out,
     brow_ref, bcol_ref, count_ref,
     block, plain, turned, row_slot, col_slot, split, spread, row_table, col_table, row_vec, slot_top, own_ids,
-    ids, row_buf, col_buf,
+    ids_row, ids, row_buf, col_buf,
     meta_sem, load_sem, ids_send_sem, ids_recv_sem,
     row_send_sem, row_recv_sem, col_send_sem, col_recv_sem,
 ):
@@ -152,20 +153,23 @@
     def one_pass(data, vec, ids_ref, slot):
         set_split(vec)
         table = row_table if ids_ref is brow_ref else col_table
-        half, pairs = few // 2, slots // 2
-        ahead = half + half // 2
-        for p in range(ahead):
-            spread_pair(ids_ref, table, p)
-            if 2 <= p < half + 2:
-                for j in range(2):
-                    scale_tile(data, 2 * (p - 2) + j, slot)
+
+        def run(n):
+            pairs = n // 2
+            for p in range(pairs + LEAD):
+                if p < pairs:
+                    spread_pair(ids_ref, table, p)
+                if p >= LEAD:
+                    for j in range(2):
+                        scale_tile(data, 2 * (p - LEAD) + j, slot)
 
         @pl.when(holder)
         def _():
-            for p in range(ahead, pairs):
-                spread_pair(ids_ref, table, p)
-            for s in range(few, slots):
-                scale_tile(data, s, slot)
+            run(slots)
+
+        @pl.when(jnp.logical_not(holder))
+        def _():
+            run(few)
 
     def gather_slots(ref, kind, where_ids, n, out):
         for h in range(halves):
@@ -188,7 +192,7 @@
 
     def ids_copies():
         return [pltpu.make_async_remote_copy(
-            src_ref=ids.at[pc], dst_ref=ids.at[pc],
+            src_ref=ids_row.at[pc], dst_ref=ids_row.at[pc],
             send_sem=ids_send_sem.at[m - 1], recv_sem=ids_recv_sem.at[pc],
             device_id={"pcol": partner(pc, m, n_pcol)},
         ) for m in range(n_pcol - 1, 0, -1)]
@@ -229,11 +233,29 @@
     def arrived(copy):
         copy.wait_recv()
 
+    per = n_pcol // group
+
+    def place(i):
+        return lax.rem(lax.rem(pr, group) + 1 + lax.div(i, per), group) + group * lax.rem(i, per)
+
+    def wait_ids():
+        for i in range(n_pcol - per):
+            q = place(i)
+
+            @pl.when(q != pc)
+            def _():
+                pltpu.make_async_remote_copy(
+                    src_ref=ids_row.at[q], dst_ref=ids_row.at[q], send_sem=ids_send_sem.at[0],
+                    recv_sem=ids_recv_sem.at[q], device_id={"pcol": q},
+                ).wait_recv()
+
+        for i in range(n_pcol - per):
+            q = place(i)
+            own = jnp.where(part == slot_of, jnp.broadcast_to(ids_row[q], (few, LANES)), -1)
+            own = jnp.max(own.astype(jnp.float32), axis=1, keepdims=True)
+            ids[q] = jnp.broadcast_to(own, (few, LANES)).astype(jnp.int32)
+
     def wait_rows(k):
-        per = n_pcol // group
-
-        def place(i):
-            return lax.rem(lax.rem(pr, group) + 1 + lax.div(i, per), group) + group * lax.rem(i, per)
 
         def wait_few(i):
             q = place(i)
@@ -245,11 +267,6 @@
                     src_ref=ref, dst_ref=ref, send_sem=row_send_sem.at[k, 0],
                     recv_sem=row_recv_sem.at[k, q], device_id={"pcol": q},
                 ).wait_recv()
-                if k == 0:
-                    pltpu.make_async_remote_copy(
-                        src_ref=ids.at[q], dst_ref=ids.at[q], send_sem=ids_send_sem.at[0],
-                        recv_sem=ids_recv_sem.at[q], device_id={"pcol": q},
-                    ).wait_recv()
 
         def from_few(first, n, acc):
             for i in range(n):
@@ -300,19 +317,31 @@
         for s in range(slots):
             own = jnp.where(s < count_ref[0], ref[s], -1)
             own_ids[kind, s:s + 1, :] = jnp.full((1, LANES), own, jnp.int32)
-    ids[pc] = own_ids[1, :few]
-    lax.fori_loop(0, steps, first_step, 0)
-    pl.semaphore_wait(barrier, n_pcol - 1 + n_prow - 1)
+    part = lax.broadcasted_iota(jnp.int32, (few, LANES), 1) // (LANES // few)
+    slot_of = lax.broadcasted_iota(jnp.int32, (few, LANES), 0)
+    own = jnp.where(part == slot_of, own_ids[1, :few], -1)
+    ids_row[pc] = jnp.max(own, axis=0, keepdims=True)
+    peers = n_pcol - 1 + n_prow - 1
+
+    @pl.when(holder)
+    def _():
+        lax.fori_loop(0, slots // STEP, first_step, 0)
+        pl.semaphore_wait(barrier, peers)
+
+    @pl.when(jnp.logical_not(holder))
+    def _():
+        lax.fori_loop(0, few // STEP // 2, first_step, 0)
+        pl.semaphore_wait(barrier, peers)
+        for copy in ids_copies():
+            copy.start()
+        lax.fori_loop(few // STEP // 2, few // STEP, first_step, 0)
+
     send_rows(0)
     send_cols(0)
 
-    @pl.when(jnp.logical_not(holder))
-    def _():
-        for copy in ids_copies():
-            copy.start()
-
     lax.fori_loop(0, steps * STEP, prepare, 0)
 
+    wait_ids()
     one = jnp.ones((BR_DEV, width), jnp.float32)
     row_1 = rescale(one, wait_rows(0))
     one_pass(plain, row_1, brow_ref, col_slot)
@@ -395,6 +424,7 @@
                 pltpu.VMEM((BR_DEV, width), jnp.float32),
                 pltpu.VMEM((slots, width), jnp.float32),
                 pltpu.VMEM((2, slots, LANES), jnp.int32),
+                pltpu.VMEM((n_pcol, 1, LANES), jnp.int32),
                 pltpu.VMEM((n_pcol, slots // 2, LANES), jnp.int32),
                 pltpu.VMEM((SWEEPS, n_pcol, BR_DEV, width), jnp.float32),
                 pltpu.VMEM((SWEEPS, n_prow, col_blocks, width), jnp.float32),

time: 23.5 us -> 22.7 us (0.966)
  Pallas kernels: 22.1 us -> 21.3 us
    pallas_call x1, Pallas kernels: 21.5 us -> 20.7 us  [on_device(): pl.pallas_call(functools.partial(kernel, n_prow, n_pcol, col_blocks, slot...]
where the time goes in v4:
time: 22.7 us; the launch traced here: 22.6 us
  Pallas kernels  21.3 us (94%)
  between operations  1.29 us (6%)
    pallas_call x1, Pallas kernels, on_device(): pl.pallas_call(functools.partial(kernel, n_prow, n_pcol, col_blocks, slot...  20.7 us
    pallas_call x1, Pallas kernels, on_device(): pl.pallas_call(spell, out_shape=(jax.ShapeDtypeStruct((BR_DEV, 1, width),...  0.64 us

profile of v4, /device:TPU:0, one launch (start us, length us, event | category | flops | bytes accessed | tf_op | source)
XLA Modules:
  0.0 22.6 jit_solution(8665305187605613957)
XLA Ops:
  1.3 20.7 %shard_map.59 = (f32[32,256]{1,0:T(8,128)S(1)}, f32[16,256]{1,0:T(8,128)S(1)}) custom-call(s32[32]{0:T(128)} %bitcast.6, s32[32]{0:T(128)} %bitcast.7, s32[1]{0:T(128)} %bitcast.4.count_hbm, bf16[32,256,256]{2,1,0:T(8,128)(2,1)} %bitcast.5), custom_call_target="tpu_custom_call" | custom-call | tf_op jit(solution)/shard_map/pallas_call | solution.py:403
  21.9 0.6 %shard_map.60 = (f32[32,1,256]{2,1,0:T(1,128)}, f32[16,1,256]{2,1,0:T(1,128)}) custom-call(f32[32,256]{1,0:T(8,128)S(1)} %get-tuple-element.4.row_ref, f32[16,256]{1,0:T(8,128)S(1)} %get-tuple-element.5.col_ref), custom_call_target="tpu_custom_call" | custom-call | tf_op jit(solution)/shard_map/pallas_call | solution.py:449

commit v5 on v4

--- a/solution.py
+++ b/solution.py
@@ -311,6 +311,23 @@
             ).wait_recv()
         return widest([col_buf[k, q] for q in range(n_prow)])
 
+    def sent(k):
+        @pl.when(holder)
+        def _():
+            for copy in row_copies(k, BR_DEV):
+                copy.wait_send()
+
+        @pl.when(jnp.logical_not(holder))
+        def _():
+            for copy in row_copies(k, few):
+                copy.wait_send()
+            if k == 0:
+                for copy in ids_copies():
+                    copy.wait_send()
+
+        for copy in col_copies(k):
+            copy.wait_send()
+
     for meta in metas:
         meta.wait()
     for kind, ref in enumerate((bcol_ref, brow_ref)):
@@ -336,8 +353,8 @@
             copy.start()
         lax.fori_loop(few // STEP // 2, few // STEP, first_step, 0)
 
+    send_cols(0)
     send_rows(0)
-    send_cols(0)
 
     lax.fori_loop(0, steps * STEP, prepare, 0)
 
@@ -356,6 +373,7 @@
         return carry
 
     lax.fori_loop(0, steps * STEP, scale_turned, 0)
+    sent(0)
     col_2 = rescale(col_1, col_1 * wait_cols(1))
     one_pass(turned, col_2, bcol_ref, row_slot)
     send_rows(2)
@@ -363,26 +381,11 @@
     row_2 = rescale(row_1, row_max)
     one_pass(plain, row_2, brow_ref, col_slot)
     send_cols(2)
+    for k in range(1, SWEEPS):
+        sent(k)
     change = 1.0 / jnp.sqrt(row_max)
     row_out[...] = rescale(row_2, change * wait_rows(2))
     col_out[...] = rescale(col_2, col_2 * wait_cols(2))
-
-    for k in range(SWEEPS):
-        @pl.when(holder)
-        def _():
-            for copy in row_copies(k, BR_DEV):
-                copy.wait_send()
-
-        @pl.when(jnp.logical_not(holder))
-        def _():
-            for copy in row_copies(k, few):
-                copy.wait_send()
-            if k == 0:
-                for copy in ids_copies():
-                    copy.wait_send()
-
-        for copy in col_copies(k):
-            copy.wait_send()
 
 
 def spell(row_ref, col_ref, row_out, col_out):

time: 22.7 us -> 22.8 us (level)
  no operation moved by 1% of the time
where the time goes in v5:
time: 22.8 us; the launch traced here: 22.6 us
  Pallas kernels  21.3 us (93%)
  between operations  1.29 us (6%)
    pallas_call x1, Pallas kernels, on_device(): pl.pallas_call(functools.partial(kernel, n_prow, n_pcol, col_blocks, slot...  20.7 us
    pallas_call x1, Pallas kernels, on_device(): pl.pallas_call(spell, out_shape=(jax.ShapeDtypeStruct((BR_DEV, 1, width),...  0.64 us

profile of v5, /device:TPU:0, one launch (start us, length us, event | category | flops | bytes accessed | tf_op | source)
XLA Modules:
  0.0 22.6 jit_solution(15604511658154266123)
XLA Ops:
  1.3 20.7 %shard_map.59 = (f32[32,256]{1,0:T(8,128)S(1)}, f32[16,256]{1,0:T(8,128)S(1)}) custom-call(s32[32]{0:T(128)} %bitcast.6, s32[32]{0:T(128)} %bitcast.7, s32[1]{0:T(128)} %bitcast.4.count_hbm, bf16[32,256,256]{2,1,0:T(8,128)(2,1)} %bitcast.5), custom_call_target="tpu_custom_call" | custom-call | tf_op jit(solution)/shard_map/pallas_call | solution.py:406
  22.0 0.6 %shard_map.60 = (f32[32,1,256]{2,1,0:T(1,128)}, f32[16,1,256]{2,1,0:T(1,128)}) custom-call(f32[32,256]{1,0:T(8,128)S(1)} %get-tuple-element.4.row_ref, f32[16,256]{1,0:T(8,128)S(1)} %get-tuple-element.5.col_ref), custom_call_target="tpu_custom_call" | custom-call | tf_op jit(solution)/shard_map/pallas_call | solution.py:452
